TPU v7x, 32 devices: a whole 2x2x4 slice. The times are simulated.
32 devices in a mesh: pipe: 2 (over y), dp: 4 (over z), tensor: 4 (over x, core).
Axes of the slice: x: 2, y: 2, z: 4, core: 2. Of those that a mesh axis runs over, the one named last changes fastest.
Arguments:
- saved: bfloat16 [2, 2, 256, 1024], P('pipe', None, 'dp'), may hold values from -6 to 6
- top_grad: bfloat16 [2, 256, 1024], P(None, 'dp'), may hold values from -6 to 6
- gain: bfloat16 [2, 1024], P('pipe', 'dp'), may hold values from 0.25 to 1.75
- w_query: bfloat16 [2, 1024, 1536], P('pipe', 'dp', 'tensor'), may hold values from -0.1875 to 0.1875
- w_latent: bfloat16 [2, 1024, 576], P('pipe', 'dp'), may hold values from -0.1875 to 0.1875
- compressed_gain: bfloat16 [2, 512], P('pipe', 'dp'), may hold values from 0.25 to 1.75
- expand_weight: bfloat16 [2, 512, 2048], P('pipe', 'dp', 'tensor'), may hold values from -0.25 to 0.25
- w_output: bfloat16 [2, 1024, 1024], P('pipe', 'tensor', 'dp'), may hold values from -0.1875 to 0.1875
Outputs:
- input_grad: bfloat16 [2, 2, 256, 1024], P('pipe', None, ('dp', 'tensor'))
- grad_gain: float32 [2, 1024], P('pipe', 'dp')
- grad_query: float32 [2, 1024, 1536], P('pipe', 'dp', 'tensor')
- grad_latent: float32 [2, 1024, 576], P('pipe', 'dp')
- grad_latent_gain: float32 [2, 512], P('pipe', 'dp')
- grad_expand: float32 [2, 512, 2048], P('pipe', 'dp', 'tensor')
- grad_output: float32 [2, 1024, 1024], P('pipe', 'tensor', 'dp')
All inputs are finite; a program needn't handle non-finite values.
Results may differ from a plain program's by a relative error of at most 0.04.
Values may be sent and summed in bfloat16 or wider, within the bound.
A program may use at most 64 MiB of HBM per device.

v0:
```python
import jax
import jax.numpy as jnp
from jax import lax
from jax.sharding import PartitionSpec as P

NOPE = 128
ROPE = 64
VDIM = 128
COMPRESSED_RANK = 512
EPS = 1e-06


def passed_along(value, axis, steps):
    count = lax.axis_size(axis)
    first, last = (max(0, -steps), min(count, count - steps))
    return lax.ppermute(value, axis, [(source, source + steps) for source in range(first, last)])


def root_mean_scale(values, scale):
    return values * lax.rsqrt(jnp.mean(values * values, axis=-1, keepdims=True) + EPS) * scale


def rotary_angles(values):
    length = values.shape[0]
    half = values.shape[-1] // 2
    freq = jnp.exp(-jnp.log(10000.0) * jnp.arange(half, dtype=jnp.float32) / half)
    angle = jnp.arange(length, dtype=jnp.float32)[:, None] * freq[None, :]
    cosine = jnp.cos(angle)[:, None, :]
    sine = jnp.sin(angle)[:, None, :]
    first = values[..., :half]
    second = values[..., half:]
    return jnp.concatenate(
        [first * cosine - second * sine, second * cosine + first * sine], axis=-1
    )


def branch(normed, w_q, w_lat, latent_norm_gain, w_exp, w_out):
    length = normed.shape[0]
    heads = w_q.shape[1] // (NOPE + ROPE)
    rounded = normed.astype(jnp.bfloat16)
    query = jnp.dot(rounded, w_q, preferred_element_type=jnp.float32).reshape(
        length, heads, NOPE + ROPE
    )
    latent_state = jnp.dot(rounded, w_lat, preferred_element_type=jnp.float32)
    compressed_state = root_mean_scale(latent_state[:, :COMPRESSED_RANK], latent_norm_gain).astype(
        jnp.bfloat16
    )
    rotary_key_part = rotary_angles(latent_state[:, None, COMPRESSED_RANK:])[:, 0, :]
    expanded = jnp.dot(compressed_state, w_exp, preferred_element_type=jnp.float32).reshape(
        length, heads, NOPE + VDIM
    )
    key_nope = expanded[:, :, :NOPE]
    values = expanded[:, :, NOPE:].astype(jnp.bfloat16)
    query_rope = rotary_angles(query[:, :, NOPE:])
    scores = jnp.einsum("qhd,khd->hqk", query[:, :, :NOPE], key_nope) + jnp.einsum(
        "qhd,kd->hqk", query_rope, rotary_key_part
    )
    scores = scores * (NOPE + ROPE) ** (-0.5)
    causal = jnp.arange(length)[:, None] >= jnp.arange(length)[None, :]
    scores = jnp.where(causal[None], scores, -1e30)
    weights = jax.nn.softmax(scores, axis=-1).astype(jnp.bfloat16)
    mixed = jnp.einsum("hqk,khd->qhd", weights.astype(jnp.float32), values.astype(jnp.float32))
    mixed = mixed.astype(jnp.bfloat16).reshape(length, heads * VDIM)
    return jnp.dot(mixed, w_out, preferred_element_type=jnp.float32)


def shards(saved, top_grad, gain, w_query, w_latent, compressed_gain, expand_weight, w_output):
    gathered = (
        lax.all_gather(gain, "dp", axis=1, tiled=True),
        lax.all_gather(w_query, "dp", axis=1, tiled=True),
        lax.all_gather(w_latent, "dp", axis=1, tiled=True),
        lax.all_gather(compressed_gain, "dp", axis=1, tiled=True),
        lax.all_gather(expand_weight, "dp", axis=1, tiled=True),
        lax.all_gather(w_output, "dp", axis=2, tiled=True),
    )
    gain32 = gathered[0][0].astype(jnp.float32)
    query_all = gathered[1][0]
    latent_all = gathered[2][0]
    lgain32 = gathered[3][0].astype(jnp.float32)
    expand_all = gathered[4][0]
    output_all = gathered[5][0]
    sections = lax.axis_size("pipe")
    section_index = lax.axis_index("pipe")
    tensor_count = lax.axis_size("tensor")
    tensor_rank = lax.axis_index("tensor")
    micro_count = saved.shape[1]
    length = saved.shape[2]
    width = saved.shape[3]
    share = length // tensor_count

    def compute(normed, upstream):
        unused, pull = jax.vjp(
            lambda value: branch(value, query_all, latent_all, lgain32, expand_all, output_all),
            normed,
        )
        return pull(upstream.astype(jnp.float32))[0]

    def skip(normed, upstream):
        return jnp.zeros_like(normed)

    gain_total = jnp.zeros((width,), jnp.float32)
    results = jnp.zeros((micro_count, share, width), jnp.bfloat16)
    stored = jnp.zeros((micro_count, length, width), jnp.bfloat16)
    received = jnp.zeros((length, width), jnp.bfloat16)
    for tick in range(sections + micro_count - 1):
        micro = tick - (sections - 1 - section_index)
        active = jnp.logical_and(micro >= 0, micro < micro_count)
        picked = jnp.clip(micro, 0, micro_count - 1)
        x_rows = lax.dynamic_index_in_dim(saved[0], picked, 0, keepdims=False)
        top_rows = lax.dynamic_index_in_dim(top_grad, picked, 0, keepdims=False)
        arrived = received
        upstream = jnp.where(section_index == sections - 1, top_rows, arrived)
        x_float = x_rows.astype(jnp.float32)
        normed, norm_pull = jax.vjp(root_mean_scale, x_float, gain32)
        branch_grad = lax.cond(active, compute, skip, normed, upstream)
        d_normed = lax.psum(branch_grad.astype(jnp.bfloat16), "tensor").astype(jnp.float32)
        dx_norm, d_gain = norm_pull(d_normed)
        dx = (upstream.astype(jnp.float32) + dx_norm).astype(jnp.bfloat16)
        gain_total = gain_total + jnp.where(active, d_gain, 0.0)
        mine = lax.dynamic_slice_in_dim(dx, tensor_rank * share, share, 0)
        chosen = (jnp.arange(micro_count) == micro)[:, None, None]
        results = jnp.where(chosen, mine[None], results)
        stored = jnp.where(chosen, upstream[None], stored)
        received = passed_along(dx, "pipe", -1)
    totals = (
        jnp.zeros(query_all.shape, jnp.float32),
        jnp.zeros(latent_all.shape, jnp.float32),
        jnp.zeros(lgain32.shape, jnp.float32),
        jnp.zeros(expand_all.shape, jnp.float32),
        jnp.zeros(output_all.shape, jnp.float32),
    )
    for micro_index in range(micro_count):
        normed_again = root_mean_scale(saved[0, micro_index].astype(jnp.float32), gain32)
        unused, weight_pull = jax.vjp(
            lambda w_q, w_lat, lat_gain, w_exp, w_out: branch(
                normed_again, w_q, w_lat, lat_gain, w_exp, w_out
            ),
            query_all,
            latent_all,
            lgain32,
            expand_all,
            output_all,
        )
        cotangents = weight_pull(stored[micro_index].astype(jnp.float32))
        totals = tuple(
            (total + piece.astype(jnp.float32) for total, piece in zip(totals, cotangents))
        )
    gain_part = jnp.where(tensor_rank == 0, gain_total, 0.0)
    grad_q, grad_lat, grad_lg, grad_e, grad_o = totals
    out_q, part_lat, part_lg, out_e, out_o, part_gain = (
        lax.psum_scatter(grad_q.astype(jnp.bfloat16), "dp", scatter_dimension=0, tiled=True).astype(
            jnp.float32
        ),
        lax.psum_scatter(
            grad_lat.astype(jnp.bfloat16), "dp", scatter_dimension=0, tiled=True
        ).astype(jnp.float32),
        lax.psum_scatter(
            grad_lg.astype(jnp.bfloat16), "dp", scatter_dimension=0, tiled=True
        ).astype(jnp.float32),
        lax.psum_scatter(grad_e.astype(jnp.bfloat16), "dp", scatter_dimension=0, tiled=True).astype(
            jnp.float32
        ),
        lax.psum_scatter(grad_o.astype(jnp.bfloat16), "dp", scatter_dimension=1, tiled=True).astype(
            jnp.float32
        ),
        lax.psum_scatter(
            gain_part.astype(jnp.bfloat16), "dp", scatter_dimension=0, tiled=True
        ).astype(jnp.float32),
    )
    out_lat, out_lg, out_gain = (
        lax.psum(part_lat.astype(jnp.bfloat16), "tensor").astype(jnp.float32),
        lax.psum(part_lg.astype(jnp.bfloat16), "tensor").astype(jnp.float32),
        lax.psum(part_gain.astype(jnp.bfloat16), "tensor").astype(jnp.float32),
    )
    return (
        results[None],
        out_gain[None],
        out_q[None],
        out_lat[None],
        out_lg[None],
        out_e[None],
        out_o[None],
    )


def solution(mesh):
    in_specs = (
        P("pipe", None, "dp", None),
        P(None, "dp", None),
        P("pipe", "dp"),
        P("pipe", "dp", "tensor"),
        P("pipe", "dp", None),
        P("pipe", "dp"),
        P("pipe", "dp", "tensor"),
        P("pipe", "tensor", "dp"),
    )
    out_specs = (
        P("pipe", None, ("dp", "tensor"), None),
        P("pipe", "dp"),
        P("pipe", "dp", "tensor"),
        P("pipe", "dp", None),
        P("pipe", "dp"),
        P("pipe", "dp", "tensor"),
        P("pipe", "tensor", "dp"),
    )
    return jax.shard_map(shards, mesh=mesh, in_specs=in_specs, out_specs=out_specs, check_vma=False)
```

profile of v0, /device:TPU:0, one launch (start us, length us, event | category | flops | bytes accessed | tf_op | source)
XLA Modules:
  0.0 381.7 jit_solution(9613141689715986463)
XLA Ops:
  7.2 1.9 copy.179
  9.3 12.9 %all_gather.19 = bf16[1,1024]{1,0:T(2,128)(2,1)S(1)} all-gather(bf16[1,256]{1,0:T(2,128)(2,1)} %param.16), channel_id=1, replica_groups=mesh['pipe'=2,'dp'=4,'tensor'=4] {'dp'}, dimensions={1}, use_global_device_ids=true | all-gather | bytes 2560 | tf_op jit(solution)/shard_map/all_gather | solution.py:69
  22.2 8.1 %all_gather.21 = bf16[1,512]{1,0:T(2,128)(2,1)S(1)} all-gather(bf16[1,128]{1,0:T(2,128)(2,1)} %param.19), channel_id=1, replica_groups=mesh['pipe'=2,'dp'=4,'tensor'=4] {'dp'}, dimensions={1}, use_global_device_ids=true | all-gather | bytes 1280 | tf_op jit(solution)/shard_map/all_gather | solution.py:72
  32.3 22.0 %all_gather.18 = bf16[1,256,1024]{2,1,0:T(8,128)(2,1)} all-gather(bf16[1,256,256]{2,1,0:T(8,128)(2,1)S(1)} %copy-done.55), channel_id=1, replica_groups=mesh['pipe'=2,'dp'=4,'tensor'=4] {'dp'}, dimensions={2}, use_global_device_ids=true | all-gather | bytes 655360 | tf_op jit(solution)/shard_map/all_gather | solution.py:74
  54.3 16.2 %all_gather.22 = bf16[1,512,512]{2,1,0:T(8,128)(2,1)S(1)} all-gather(bf16[1,128,512]{2,1,0:T(8,128)(2,1)S(1)} %copy-done.56), channel_id=1, replica_groups=mesh['pipe'=2,'dp'=4,'tensor'=4] {'dp'}, dimensions={1}, use_global_device_ids=true | all-gather | bytes 655360 | tf_op jit(solution)/shard_map/all_gather | solution.py:73
  71.3 17.4 %all_gather.23 = bf16[1,1024,384]{2,1,0:T(8,128)(2,1)} all-gather(bf16[1,256,384]{2,1,0:T(8,128)(2,1)S(1)} %copy-done.42), channel_id=1, replica_groups=mesh['pipe'=2,'dp'=4,'tensor'=4] {'dp'}, dimensions={1}, use_global_device_ids=true | all-gather | bytes 983040 | tf_op jit(solution)/shard_map/all_gather | solution.py:70
  89.5 40.7 %all-reduce.59.cloned.1.call-done = bf16[64,1024]{1,0:T(8,128)(2,1)} async-done(((bf16[64,1024]{1,0:T(8,128)(2,1)}), bf16[64,1024]{1,0:T(8,128)(2,1)}) %all-reduce.59.cloned.1.call-update) | async-done | bytes 131088 | tf_op jit(solution)/shard_map/psum | solution.py:116
  130.2 1.7 fusion.162
  132.5 1.9 convert_multiply_fusion.16
  138.6 2.7 collective-permute-done
  142.3 28.0 %conditional.4 = (bf16[64,1024]{1,0:T(8,128)(2,1)}) conditional(s32[]{:T(128)} %convert_element_type.460, () %tuple.34, (bf16[64,1024]{1,0:T(8,128)(2,1)S(1)}, bf16[256,1024]{1,0:T(8,128)(2,1)}, f32[1024]{0:T(1024)S(1)}, f32[64,1024]{1,0:T(8,128)}, bf16[1024,576]{1,0:T(8,128)(2,1)S(1)}, /*index=5*/f32[512]{0:T(512)S(1)}, ...), branch_computations={%region_11.12_spmd, %region_12.0_spmd} | conditional | flops 367509920 | bytes 12992140 | solution.py:115
  142.3 2.0 fusion.75
  144.3 2.0 fusion.74
  146.3 1.7 reshape.749
  155.8 1.8 fusion.56
  166.5 1.6 reshape.751
  168.0 2.2 fusion.47
  170.8 30.4 %all-reduce.61.cloned.1.call-done = bf16[64,1024]{1,0:T(8,128)(2,1)} async-done(((bf16[64,1024]{1,0:T(8,128)(2,1)}), bf16[64,1024]{1,0:T(8,128)(2,1)}) %all-reduce.61.cloned.1.call-update) | async-done | bytes 131088 | tf_op jit(solution)/shard_map/psum | solution.py:116
  201.3 1.6 fusion.163
  210.2 1.7 collective-permute-done.1
  225.0 1.6 add_convert_fusion
  236.1 9.3 %conditional.5 = (bf16[64,1024]{1,0:T(8,128)(2,1)S(1)}) conditional(s32[]{:T(128)} %convert_element_type.467, () %tuple.36, (bf16[64,1024]{1,0:T(8,128)(2,1)S(1)}, bf16[256,1024]{1,0:T(8,128)(2,1)}, f32[1024]{0:T(1024)S(1)}, f32[64,1024]{1,0:T(8,128)S(1)}, bf16[1024,576]{1,0:T(8,128)(2,1)S(1)}, /*index=5*/f32[512]{0:T(512)S(1)}, ...), branch_computations={%region_21.22_spmd, %region_22.28_spmd} | conditional | flops 367509920 | bytes 10745208 | solution.py:115
  246.2 1.6 bitcast_convert_fusion.2
  247.8 15.5 %reduce-scatter.11.cloned.1.call-done = bf16[256,256]{1,0:T(8,128)(2,1)} async-done(((bf16[256,1024]{1,0:T(8,128)(2,1)}), bf16[256,256]{1,0:T(8,128)(2,1)}) %reduce-scatter.11.cloned.1.call-update) | async-done | bytes 131088 | tf_op jit(solution)/shard_map/reduce_scatter | solution.py:163
  263.3 1.6 bitcast_convert_fusion.1
  264.9 28.1 %reduce-scatter.7.cloned.1.call-done = bf16[256,576]{0,1:T(8,128)(2,1)} async-done(((bf16[1024,576]{0,1:T(8,128)(2,1)}), bf16[256,576]{0,1:T(8,128)(2,1)}) %reduce-scatter.7.cloned.1.call-update) | async-done | bytes 294928 | tf_op jit(solution)/shard_map/reduce_scatter | solution.py:154
  293.1 24.0 %reduce-scatter.5.cloned.1.call-done = bf16[256,384]{1,0:T(8,128)(2,1)} async-done(((bf16[1024,384]{1,0:T(8,128)(2,1)}), bf16[256,384]{1,0:T(8,128)(2,1)}) %reduce-scatter.5.cloned.1.call-update) | async-done | bytes 196624 | tf_op jit(solution)/shard_map/reduce_scatter | solution.py:151
  317.2 1.7 bitcast_convert_fusion
  318.9 33.2 %all-reduce.63.cloned.1.call-done = (bf16[64,1024]{1,0:T(8,128)(2,1)}, bf16[1,256,576]{1,2,0:T(8,128)(2,1)}) async-done(((bf16[64,1024]{1,0:T(8,128)(2,1)}, bf16[1,256,576]{1,2,0:T(8,128)(2,1)}), (bf16[64,1024]{1,0:T(8,128)(2,1)}, bf16[1,256,576]{1,2,0:T(8,128)(2,1)})) %all-reduce.63.cloned.1.call-update) | async-done | bytes 426000 | tf_op jit(solution)/shard_map/psum | solution.py:116
  353.4 11.7 %all-reduce.54 = (bf16[1024]{0:T(1024)(128)(2,1)S(1)}, bf16[512]{0:T(512)(128)(2,1)S(1)}) all-reduce(bf16[1024]{0:T(1024)(128)(2,1)S(1)} %select_convert_fusion, bf16[512]{0:T(512)(128)(2,1)S(1)} %add_convert_fusion.2), channel_id=2, replica_groups=mesh['pipe'=2,'dp'=4,'tensor'=4] {'dp'}, use_global_device_ids=true, to_apply=%region_33.34.clone | all-reduce | flops 1536 | bytes 6144
  365.2 5.9 %all-reduce.52 = (bf16[1,256]{1,0:T(2,128)(2,1)S(1)}, bf16[1,128]{1,0:T(2,128)(2,1)S(1)}) all-reduce(bf16[1,256]{1,0:T(2,128)(2,1)S(1)} %broadcast_in_dim.412, bf16[1,128]{1,0:T(2,128)(2,1)S(1)} %dynamic-slice_bitcast_fusion), channel_id=1, replica_groups=mesh['pipe'=2,'dp'=4,'tensor'=4] {'tensor'}, use_global_device_ids=true, to_apply=%region_34.35 | all-reduce | flops 384 | bytes 1536 | tf_op jit(solution)/shard_map/psum | solution.py:173
  371.6 1.8 broadcast_in_dim.440
  (451 shorter events, 66.9 us)
Async XLA Ops:
  7.2 64.1 %copy-start.2 = (bf16[1,2,64,1024]{3,2,1,0:T(8,128)(2,1)S(1)}, bf16[1,2,64,1024]{3,2,1,0:T(8,128)(2,1)}, u32[]{:S(2)}) copy-start(bf16[1,2,64,1024]{3,2,1,0:T(8,128)(2,1)} %param.14) | copy-start | bytes 786436
  7.2 25.1 %copy-start.55 = (bf16[1,256,256]{2,1,0:T(8,128)(2,1)S(1)}, bf16[1,256,256]{2,1,0:T(8,128)(2,1)}, u32[]{:S(2)}) copy-start(bf16[1,256,256]{2,1,0:T(8,128)(2,1)} %param.21) | copy-start | bytes 393220
  7.2 47.1 %copy-start.56 = (bf16[1,128,512]{2,1,0:T(8,128)(2,1)S(1)}, bf16[1,128,512]{2,1,0:T(8,128)(2,1)}, u32[]{:S(2)}) copy-start(bf16[1,128,512]{2,1,0:T(8,128)(2,1)} %param.20) | copy-start | bytes 393220
  7.2 81.5 %all-gather.2.cloned.1.call-start = ((), (), s32[]{:S(2)}) async-start(), calls=%async_computation.4 | async-start | bytes 1638400 | tf_op jit(solution)/shard_map/all_gather | solution.py:71
  9.2 62.2 %copy-start.42 = (bf16[1,256,384]{2,1,0:T(8,128)(2,1)S(1)}, bf16[1,256,384]{2,1,0:T(8,128)(2,1)}, u32[]{:S(2)}) copy-start(bf16[1,256,384]{2,1,0:T(8,128)(2,1)} %param.17) | copy-start | bytes 589828
  9.2 121.0 %all-reduce.59.cloned.1.call-start = ((), (), s32[]{:S(2)}) async-start(), calls=%async_computation.5 | async-start | bytes 262144 | tf_op jit(solution)/shard_map/psum | solution.py:116
  31.4 57.3 %copy-start.84 = (f32[32]{0:T(128)}, f32[32]{0:T(128)S(1)}, u32[]{:S(2)}) copy-start(f32[32]{0:T(128)S(1)} %multiply_exponential_fusion.3) | copy-start | bytes 388
  32.3 56.4 %copy-start.8 = (bf16[64,1024]{1,0:T(8,128)(2,1)}, bf16[64,1024]{1,0:T(8,128)(2,1)S(1)}, u32[]{:S(2)}) copy-start(bf16[64,1024]{1,0:T(8,128)(2,1)S(1)} %select_bitcast_fusion) | copy-start | bytes 393220
  88.7 43.7 %copy-start.10 = (bf16[2,64,1024]{2,1,0:T(8,128)(2,1)S(1)}, bf16[2,64,1024]{2,1,0:T(8,128)(2,1)}, u32[]{:S(2)}) copy-start(bf16[2,64,1024]{2,1,0:T(8,128)(2,1)} %param.15) | copy-start | bytes 786436
  89.5 111.8 %all-reduce.61.cloned.1.call-start = ((), (), s32[]{:S(2)}) async-start(), calls=%async_computation.6 | async-start | bytes 262144 | tf_op jit(solution)/shard_map/psum | solution.py:116
  134.3 7.0 %collective-permute-start = (bf16[64,1024]{1,0:T(8,128)(2,1)S(1)}, bf16[64,1024]{1,0:T(8,128)(2,1)}, u32[]{:S(2)}, u32[]{:S(2)}) collective-permute-start(bf16[64,1024]{1,0:T(8,128)(2,1)S(1)} %get-tuple-element.188), channel_id=1, source_target_pairs={{16,0},{17,1},{18,2},{19,3},{20,4},{21,5},{22,6},{23,7},{24,8},{25... | collective-permute-start | bytes 393224 | tf_op jit(solution)/shard_map/ppermute | solution.py:16
  170.3 75.9 %reduce-scatter.9.cloned.1.call-start = ((), (), s32[]{:S(2)}) async-start(), calls=%async_computation.9 | async-start | bytes 655360 | tf_op jit(solution)/shard_map/reduce_scatter | solution.py:160
  203.3 14.5 %copy-start.3 = (f32[64,576]{1,0:T(8,128)}, f32[64,576]{1,0:T(8,128)S(1)}, u32[]{:S(2)}) copy-start(f32[64,576]{1,0:T(8,128)S(1)} %fusion.199) | copy-start | bytes 442372
  205.1 6.9 %collective-permute-start.1 = (bf16[64,1024]{1,0:T(8,128)(2,1)S(1)}, bf16[64,1024]{1,0:T(8,128)(2,1)S(1)}, u32[]{:S(2)}, u32[]{:S(2)}) collective-permute-start(bf16[64,1024]{1,0:T(8,128)(2,1)S(1)} %fusion.178), channel_id=1, source_target_pairs={{16,0},{17,1},{18,2},{19,3},{20,4},{21,5},{22,6},{23,7},{24,8},{25... | collective-permute-start | bytes 393224 | tf_op jit(solution)/shard_map/ppermute | solution.py:16
  206.6 11.3 %copy-start.81 = (f32[64]{0:T(128)}, f32[64]{0:T(128)S(1)}, u32[]{:S(2)}) copy-start(f32[64]{0:T(128)S(1)} %fusion.264) | copy-start | bytes 772
  206.7 11.6 %copy-start.83 = (f32[64]{0:T(128)}, f32[64]{0:T(128)S(1)}, u32[]{:S(2)}) copy-start(f32[64]{0:T(128)S(1)} %fusion.265) | copy-start | bytes 772
  207.3 8.9 %copy-start.34 = (bf16[64,2,256]{2,0,1:T(8,128)(2,1)}, bf16[64,2,256]{2,0,1:T(8,128)(2,1)S(1)}, u32[]{:S(2)}) copy-start(bf16[64,2,256]{2,0,1:T(8,128)(2,1)S(1)} %fusion.231) | copy-start | bytes 196612
  219.5 43.8 %reduce-scatter.11.cloned.1.call-start = ((), (), s32[]{:S(2)}) async-start(), calls=%async_computation.10 | async-start | bytes 655360 | tf_op jit(solution)/shard_map/reduce_scatter | solution.py:163
  223.4 69.7 %reduce-scatter.7.cloned.1.call-start = ((), (), s32[]{:S(2)}) async-start(), calls=%async_computation.8 | async-start | bytes 1474560 | tf_op jit(solution)/shard_map/reduce_scatter | solution.py:154
  226.7 90.4 %reduce-scatter.5.cloned.1.call-start = ((), (), s32[]{:S(2)}) async-start(), calls=%async_computation.7 | async-start | bytes 983040 | tf_op jit(solution)/shard_map/reduce_scatter | solution.py:151
  230.6 121.5 %all-reduce.63.cloned.1.call-start = ((), (), s32[]{:S(2)}) async-start(), calls=%async_computation.11 | async-start | bytes 851968 | tf_op jit(solution)/shard_map/psum | solution.py:116
  245.4 47.7 %copy-start.15 = (bf16[64,1024]{1,0:T(8,128)(2,1)}, bf16[64,1024]{1,0:T(8,128)(2,1)S(1)}, u32[]{:S(2)}) copy-start(bf16[64,1024]{1,0:T(8,128)(2,1)S(1)} %get-tuple-element.243) | copy-start | bytes 393220
  245.4 106.7 %copy-start.97 = (f32[64]{0:T(128)S(1)}, f32[64]{0:T(128)}, u32[]{:S(2)}) copy-start(f32[64]{0:T(128)} %copy-done.95) | copy-start | bytes 772
  245.4 107.8 %copy-start.111 = (f32[64]{0:T(128)S(1)}, f32[64]{0:T(128)}, u32[]{:S(2)}) copy-start(f32[64]{0:T(128)} %copy-done.110) | copy-start | bytes 772
  245.4 107.9 %copy-start.64 = (f32[1024]{0:T(1024)S(1)}, f32[1024]{0:T(1024)}, u32[]{:S(2)}) copy-start(f32[1024]{0:T(1024)} %get-tuple-element.94) | copy-start | bytes 12292
  245.4 107.9 %copy-start.65 = (f32[1024]{0:T(1024)S(1)}, f32[1024]{0:T(1024)}, u32[]{:S(2)}) copy-start(f32[1024]{0:T(1024)} %get-tuple-element.96) | copy-start | bytes 12292
  264.9 109.0 %copy-start.112 = (f32[16]{0:T(128)S(1)}, f32[16]{0:T(128)}, u32[]{:S(2)}) copy-start(f32[16]{0:T(128)} %dynamic-slice.7) | copy-start | bytes 196
  293.1 81.0 %copy-start.57 = (bf16[16,1024]{1,0:T(8,128)(2,1)S(1)}, bf16[16,1024]{1,0:T(8,128)(2,1)}, u32[]{:S(2)}) copy-start(bf16[16,1024]{1,0:T(8,128)(2,1)} %constant_dynamic-slice_fusion) | copy-start | bytes 98308
  293.1 81.0 %copy-start.58 = (bf16[16,1024]{1,0:T(8,128)(2,1)S(1)}, bf16[16,1024]{1,0:T(8,128)(2,1)}, u32[]{:S(2)}) copy-start(bf16[16,1024]{1,0:T(8,128)(2,1)} %constant_dynamic-slice_fusion.1) | copy-start | bytes 98308
  293.1 81.0 %copy-start.92 = (pred[2]{0:T(512)(128)(4,1)S(1)}, pred[2]{0:T(512)(128)(4,1)}, u32[]{:S(2)}) copy-start(pred[2]{0:T(512)(128)(4,1)} %get-tuple-element.237) | copy-start | bytes 10
  293.1 81.0 %copy-start.94 = (pred[2]{0:T(512)(128)(4,1)S(1)}, pred[2]{0:T(512)(128)(4,1)}, u32[]{:S(2)}) copy-start(pred[2]{0:T(512)(128)(4,1)} %get-tuple-element.238) | copy-start | bytes 10
  293.1 81.0 %copy-start.105 = (pred[2]{0:T(512)(128)(4,1)S(1)}, pred[2]{0:T(512)(128)(4,1)}, u32[]{:S(2)}) copy-start(pred[2]{0:T(512)(128)(4,1)} %iota_compare_fusion.10) | copy-start | bytes 10
  (97 other events, 230.3 us)
Sparse Core Ops, SparseCore 0:
  10.1 43.6 all-gather.1
  89.6 40.6 all-reduce.58
  170.4 30.8 all-reduce.60
  219.7 21.2 reduce-scatter.8
  243.0 20.2 reduce-scatter.10
  265.5 27.5 reduce-scatter.6
  295.4 21.7 reduce-scatter.4
  319.6 32.4 all-reduce.62
where the time goes:
time: 383 us; the launch traced here: 382 us
  waiting for transfers between devices  177 us (46%)
  blocking collectives  94.1 us (25%)
  matrix products  39 us (10%)
  other arithmetic  28 us (7%)
  local copies, waits for them, and re-layouts  23.4 us (6%)
  between operations  16.9 us (4%)
    psum x3, waiting for transfers between devices, shards(): lax.psum(branch_grad.astype(jnp.bfloat16), 'tensor').astype(jnp.float32)  104 us
    reduce_scatter x1, waiting for transfers between devices, shards(): lax.psum_scatter(grad_lat.astype(jnp.bfloat16), 'dp', scatter_dimension=0...  28.1 us
    reduce_scatter x1, waiting for transfers between devices, shards(): lax.psum_scatter(grad_q.astype(jnp.bfloat16), 'dp', scatter_dimension=0,...  24 us
    all_gather x1, blocking collectives, shards(): lax.all_gather(w_output, 'dp', axis=2, tiled=True)  22 us
    all_gather x1, blocking collectives, shards(): lax.all_gather(w_query, 'dp', axis=1, tiled=True)  17.4 us
    all_gather x1, blocking collectives, shards(): lax.all_gather(expand_weight, 'dp', axis=1, tiled=True)  16.2 us
    reduce_scatter x1, waiting for transfers between devices, shards(): lax.psum_scatter(grad_o.astype(jnp.bfloat16), 'dp', scatter_dimension=1,...  15.5 us
    all_gather x1, blocking collectives, shards(): lax.all_gather(gain, 'dp', axis=1, tiled=True)  12.9 us
  transfers between devices with their start and end apart: 10, of which 8 were waited for; matrix products, arithmetic and copies ran while one was open for 10% of the time, Pallas kernels for 0%

commit v1 on v0

--- a/solution.py
+++ b/solution.py
@@ -8,6 +8,7 @@
 VDIM = 128
 COMPRESSED_RANK = 512
 EPS = 1e-06
+ways_recover = lambda q_in, comm_axis: jnp.sum(jax.lax.all_gather(q_in, axis_name=comm_axis), 0)
 
 
 def passed_along(value, axis, steps):
@@ -113,7 +114,7 @@
         x_float = x_rows.astype(jnp.float32)
         normed, norm_pull = jax.vjp(root_mean_scale, x_float, gain32)
         branch_grad = lax.cond(active, compute, skip, normed, upstream)
-        d_normed = lax.psum(branch_grad.astype(jnp.bfloat16), "tensor").astype(jnp.float32)
+        d_normed = ways_recover(branch_grad.astype(jnp.bfloat16), "tensor").astype(jnp.float32)
         dx_norm, d_gain = norm_pull(d_normed)
         dx = (upstream.astype(jnp.float32) + dx_norm).astype(jnp.bfloat16)
         gain_total = gain_total + jnp.where(active, d_gain, 0.0)

time: 383 us -> 319 us (0.83)
  waiting for transfers between devices: 177 us -> 93.8 us
  blocking collectives: 94.1 us -> 114 us
    psum x3 -> x1, waiting for transfers between devices: 104 us -> 32.5 us  [shards(): lax.psum(part_lat.astype(jnp.bfloat16), 'tensor').astype(jnp.float32)]
    all_gather x0 -> x3, blocking collectives: none -> 22 us  [jax.lax.all_gather(q_in, axis_name=comm_axis)]
    reduce_scatter x1, waiting for transfers between devices: 15.5 us -> 0.01 us  [shards(): lax.psum_scatter(grad_o.astype(jnp.bfloat16), 'dp', scatter_dimension=1,...]
    ppermute x2, waiting for transfers between devices: 4.45 us -> 15.3 us  [passed_along(): lax.ppermute(value, axis, [(source, source + steps) for source in range(f...]
    reduce_scatter x1, waiting for transfers between devices: 28.1 us -> 22 us  [shards(): lax.psum_scatter(grad_lat.astype(jnp.bfloat16), 'dp', scatter_dimension=0...]
  transfers between devices with their start and end apart: 10 -> 8, of which waited for: 8 -> 5; matrix products, arithmetic and copies ran while one was open for 10% -> 12% of each run, Pallas kernels for 0% -> 0%
where the time goes in v1:
time: 319 us; the launch traced here: 318 us
  blocking collectives  114 us (36%)
  waiting for transfers between devices  93.8 us (29%)
  matrix products  39.4 us (12%)
  other arithmetic  28.7 us (9%)
  local copies, waits for them, and re-layouts  21.6 us (7%)
  between operations  16.8 us (5%)
    psum x1, waiting for transfers between devices, shards(): lax.psum(part_lat.astype(jnp.bfloat16), 'tensor').astype(jnp.float32)  32.5 us
    reduce_scatter x1, waiting for transfers between devices, shards(): lax.psum_scatter(grad_q.astype(jnp.bfloat16), 'dp', scatter_dimension=0,...  23.9 us
    reduce_scatter x1, waiting for transfers between devices, shards(): lax.psum_scatter(grad_lat.astype(jnp.bfloat16), 'dp', scatter_dimension=0...  22 us
    all_gather x3, blocking collectives, jax.lax.all_gather(q_in, axis_name=comm_axis)  22 us
    all_gather x1, blocking collectives, shards(): lax.all_gather(w_output, 'dp', axis=2, tiled=True)  21.2 us
    all_gather x1, blocking collectives, shards(): lax.all_gather(w_query, 'dp', axis=1, tiled=True)  17.5 us
    all_gather x1, blocking collectives, shards(): lax.all_gather(expand_weight, 'dp', axis=1, tiled=True)  16.2 us
    ppermute x2, waiting for transfers between devices, passed_along(): lax.ppermute(value, axis, [(source, source + steps) for source in range(f...  15.3 us
  transfers between devices with their start and end apart: 8, of which 5 were waited for; matrix products, arithmetic and copies ran while one was open for 12% of the time, Pallas kernels for 0%

profile of v1, /device:TPU:0, one launch (start us, length us, event | category | flops | bytes accessed | tf_op | source)
XLA Modules:
  0.0 317.6 jit_solution(11545357821090042736)
XLA Ops:
  7.2 1.9 copy.179
  9.9 12.9 %all_gather.37 = bf16[1,1024]{1,0:T(2,128)(2,1)S(1)} all-gather(bf16[1,256]{1,0:T(2,128)(2,1)} %param.16), channel_id=1, replica_groups=mesh['pipe'=2,'dp'=4,'tensor'=4] {'dp'}, dimensions={1}, use_global_device_ids=true | all-gather | bytes 2560 | tf_op jit(solution)/shard_map/all_gather | solution.py:70
  22.8 8.1 %all_gather.39 = bf16[1,512]{1,0:T(2,128)(2,1)S(1)} all-gather(bf16[1,128]{1,0:T(2,128)(2,1)} %param.19), channel_id=1, replica_groups=mesh['pipe'=2,'dp'=4,'tensor'=4] {'dp'}, dimensions={1}, use_global_device_ids=true | all-gather | bytes 1280 | tf_op jit(solution)/shard_map/all_gather | solution.py:73
  34.2 21.2 %all_gather.36 = bf16[1,256,1024]{2,1,0:T(8,128)(2,1)} all-gather(bf16[1,256,256]{2,1,0:T(8,128)(2,1)S(1)} %copy-done.49), channel_id=1, replica_groups=mesh['pipe'=2,'dp'=4,'tensor'=4] {'dp'}, dimensions={2}, use_global_device_ids=true | all-gather | bytes 655360 | tf_op jit(solution)/shard_map/all_gather | solution.py:75
  55.4 16.2 %all_gather.40 = bf16[1,512,512]{2,1,0:T(8,128)(2,1)S(1)} all-gather(bf16[1,128,512]{2,1,0:T(8,128)(2,1)S(1)} %copy-done.50), channel_id=1, replica_groups=mesh['pipe'=2,'dp'=4,'tensor'=4] {'dp'}, dimensions={1}, use_global_device_ids=true | all-gather | bytes 655360 | tf_op jit(solution)/shard_map/all_gather | solution.py:74
  72.5 17.5 %all_gather.41 = bf16[1,1024,384]{2,1,0:T(8,128)(2,1)} all-gather(bf16[1,256,384]{2,1,0:T(8,128)(2,1)S(1)} %copy-done.36), channel_id=1, replica_groups=mesh['pipe'=2,'dp'=4,'tensor'=4] {'dp'}, dimensions={1}, use_global_device_ids=true | all-gather | bytes 983040 | tf_op jit(solution)/shard_map/all_gather | solution.py:71
  90.0 7.0 %all-gather = bf16[256,1024]{1,0:T(8,128)(2,1)S(1)} all-gather(bf16[64,1024]{1,0:T(8,128)(2,1)S(1)} %get-tuple-element.237), channel_id=2, replica_groups=mesh['pipe'=2,'dp'=4,'tensor'=4] {'tensor'}, dimensions={0}, use_global_device_ids=true | all-gather | bytes 655360 | tf_op jit(solution)/shard_map/all_gather | solution.py:11
  107.5 9.2 %collective-permute-done = bf16[64,1024]{1,0:T(8,128)(2,1)} collective-permute-done((bf16[64,1024]{1,0:T(8,128)(2,1)S(1)}, bf16[64,1024]{1,0:T(8,128)(2,1)}, u32[]{:S(2)}, u32[]{:S(2)}) %collective-permute-start) | collective-permute-done | bytes 131104 | tf_op jit(solution)/shard_map/ppermute | solution.py:17
  117.7 28.0 %conditional.4 = (bf16[64,1024]{1,0:T(8,128)(2,1)}) conditional(s32[]{:T(128)} %convert_element_type.466, () %tuple.34, (bf16[64,1024]{1,0:T(8,128)(2,1)S(1)}, bf16[256,1024]{1,0:T(8,128)(2,1)}, f32[1024]{0:T(1024)S(1)}, f32[64,1024]{1,0:T(8,128)}, bf16[1024,576]{1,0:T(8,128)(2,1)S(1)}, /*index=5*/f32[512]{0:T(512)S(1)}, ...), branch_computations={%region_11.12_spmd, %region_12.0_spmd} | conditional | flops 367509920 | bytes 12992140 | solution.py:116
  117.7 2.0 fusion.75
  119.7 2.0 fusion.74
  121.8 1.7 reshape.749
  131.2 1.8 fusion.56
  141.9 1.6 reshape.751
  143.5 2.2 fusion.47
  145.6 8.0 %all-gather.1 = bf16[256,1024]{1,0:T(8,128)(2,1)} all-gather(bf16[64,1024]{1,0:T(8,128)(2,1)} %get-tuple-element.238), channel_id=3, replica_groups=mesh['pipe'=2,'dp'=4,'tensor'=4] {'tensor'}, dimensions={0}, use_global_device_ids=true | all-gather | bytes 655360 | tf_op jit(solution)/shard_map/all_gather | solution.py:11
  153.6 1.8 reduce_sum.377
  155.4 1.7 fusion.163
  165.2 6.1 %collective-permute-done.1 = bf16[64,1024]{1,0:T(8,128)(2,1)S(1)} collective-permute-done((bf16[64,1024]{1,0:T(8,128)(2,1)S(1)}, bf16[64,1024]{1,0:T(8,128)(2,1)S(1)}, u32[]{:S(2)}, u32[]{:S(2)}) %collective-permute-start.1) | collective-permute-done | bytes 131104 | tf_op jit(solution)/shard_map/ppermute | solution.py:17
  179.3 1.8 multiply_reduce_fusion.11
  184.7 1.6 add_convert_fusion
  186.4 9.1 %conditional.5 = (bf16[64,1024]{1,0:T(8,128)(2,1)S(1)}) conditional(s32[]{:T(128)} %convert_element_type.473, () %tuple.36, (bf16[64,1024]{1,0:T(8,128)(2,1)S(1)}, bf16[256,1024]{1,0:T(8,128)(2,1)}, f32[1024]{0:T(1024)S(1)}, f32[64,1024]{1,0:T(8,128)S(1)}, bf16[1024,576]{1,0:T(8,128)(2,1)S(1)}, /*index=5*/f32[512]{0:T(512)S(1)}, ...), branch_computations={%region_21.22_spmd, %region_22.28_spmd} | conditional | flops 367509920 | bytes 10742024 | solution.py:116
  195.6 7.0 %all-gather.2 = bf16[256,1024]{1,0:T(8,128)(2,1)S(1)} all-gather(bf16[64,1024]{1,0:T(8,128)(2,1)S(1)} %get-tuple-element.239), channel_id=4, replica_groups=mesh['pipe'=2,'dp'=4,'tensor'=4] {'tensor'}, dimensions={0}, use_global_device_ids=true | all-gather | bytes 655360 | tf_op jit(solution)/shard_map/all_gather | solution.py:11
  206.7 10.2 %all-reduce.53 = (bf16[1024]{0:T(1024)(128)(2,1)S(1)}, bf16[512]{0:T(512)(128)(2,1)S(1)}) all-reduce(bf16[1024]{0:T(1024)(128)(2,1)S(1)} %select_convert_fusion, bf16[512]{0:T(512)(128)(2,1)S(1)} %add_convert_fusion.2), channel_id=5, replica_groups=mesh['pipe'=2,'dp'=4,'tensor'=4] {'dp'}, use_global_device_ids=true, to_apply=%region_33.34.clone | all-reduce | flops 1536 | bytes 6144
  217.1 5.6 %all-reduce.52 = (bf16[1,256]{1,0:T(2,128)(2,1)S(1)}, bf16[1,128]{1,0:T(2,128)(2,1)S(1)}) all-reduce(bf16[1,256]{1,0:T(2,128)(2,1)S(1)} %broadcast_in_dim.412, bf16[1,128]{1,0:T(2,128)(2,1)S(1)} %dynamic-slice_bitcast_fusion), channel_id=1, replica_groups=mesh['pipe'=2,'dp'=4,'tensor'=4] {'tensor'}, use_global_device_ids=true, to_apply=%region_34.35 | all-reduce | flops 384 | bytes 1536 | tf_op jit(solution)/shard_map/psum | solution.py:174
  225.5 1.6 bitcast_convert_fusion.2
  227.1 1.6 bitcast_convert_fusion.1
  228.8 22.0 %reduce-scatter.7.cloned.1.call-done = bf16[256,576]{0,1:T(8,128)(2,1)} async-done(((bf16[1024,576]{0,1:T(8,128)(2,1)}), bf16[256,576]{0,1:T(8,128)(2,1)}) %reduce-scatter.7.cloned.1.call-update) | async-done | bytes 294928 | tf_op jit(solution)/shard_map/reduce_scatter | solution.py:155
  250.8 23.9 %reduce-scatter.5.cloned.1.call-done = bf16[256,384]{1,0:T(8,128)(2,1)} async-done(((bf16[1024,384]{1,0:T(8,128)(2,1)}), bf16[256,384]{1,0:T(8,128)(2,1)}) %reduce-scatter.5.cloned.1.call-update) | async-done | bytes 196624 | tf_op jit(solution)/shard_map/reduce_scatter | solution.py:152
  274.7 1.7 bitcast_convert_fusion
  276.4 32.5 %all-reduce.56.cloned.1.call-done = bf16[1,256,576]{1,2,0:T(8,128)(2,1)} async-done(((bf16[1,256,576]{1,2,0:T(8,128)(2,1)}), bf16[1,256,576]{1,2,0:T(8,128)(2,1)}) %all-reduce.56.cloned.1.call-update) | async-done | bytes 294928 | tf_op jit(solution)/shard_map/psum | solution.py:172
  308.9 1.8 broadcast_in_dim.440
  (435 shorter events, 66.0 us)
Async XLA Ops:
  7.2 26.3 %copy-start.2 = (bf16[1,2,64,1024]{3,2,1,0:T(8,128)(2,1)S(1)}, bf16[1,2,64,1024]{3,2,1,0:T(8,128)(2,1)}, u32[]{:S(2)}) copy-start(bf16[1,2,64,1024]{3,2,1,0:T(8,128)(2,1)} %param.14) | copy-start | bytes 786436
  7.2 27.1 %copy-start.49 = (bf16[1,256,256]{2,1,0:T(8,128)(2,1)S(1)}, bf16[1,256,256]{2,1,0:T(8,128)(2,1)}, u32[]{:S(2)}) copy-start(bf16[1,256,256]{2,1,0:T(8,128)(2,1)} %param.21) | copy-start | bytes 393220
  7.2 48.2 %copy-start.50 = (bf16[1,128,512]{2,1,0:T(8,128)(2,1)S(1)}, bf16[1,128,512]{2,1,0:T(8,128)(2,1)}, u32[]{:S(2)}) copy-start(bf16[1,128,512]{2,1,0:T(8,128)(2,1)} %param.20) | copy-start | bytes 393220
  7.2 82.7 %all-gather.5.cloned.1.call-start = ((), (), s32[]{:S(2)}) async-start(), calls=%async_computation.4 | async-start | bytes 1638400 | tf_op jit(solution)/shard_map/all_gather | solution.py:72
  9.2 216.3 %reduce-scatter.9.cloned.1.call-start = ((), (), s32[]{:S(2)}) async-start(), calls=%async_computation.8 | async-start | bytes 655360 | tf_op jit(solution)/shard_map/reduce_scatter | solution.py:161
  9.3 63.2 %copy-start.36 = (bf16[1,256,384]{2,1,0:T(8,128)(2,1)S(1)}, bf16[1,256,384]{2,1,0:T(8,128)(2,1)}, u32[]{:S(2)}) copy-start(bf16[1,256,384]{2,1,0:T(8,128)(2,1)} %param.17) | copy-start | bytes 589828
  9.9 80.1 %copy-start.82 = (f32[32]{0:T(128)}, f32[32]{0:T(128)S(1)}, u32[]{:S(2)}) copy-start(f32[32]{0:T(128)S(1)} %multiply_exponential_fusion.3) | copy-start | bytes 388
  33.5 56.4 %copy-start.9 = (bf16[64,1024]{1,0:T(8,128)(2,1)}, bf16[64,1024]{1,0:T(8,128)(2,1)S(1)}, u32[]{:S(2)}) copy-start(bf16[64,1024]{1,0:T(8,128)(2,1)S(1)} %select_bitcast_fusion) | copy-start | bytes 393220
  99.5 17.2 %collective-permute-start = (bf16[64,1024]{1,0:T(8,128)(2,1)S(1)}, bf16[64,1024]{1,0:T(8,128)(2,1)}, u32[]{:S(2)}, u32[]{:S(2)}) collective-permute-start(bf16[64,1024]{1,0:T(8,128)(2,1)S(1)} %get-tuple-element.186), channel_id=1, source_target_pairs={{16,0},{17,1},{18,2},{19,3},{20,4},{21,5},{22,6},{23,7},{24,8},{25... | collective-permute-start | bytes 393224 | tf_op jit(solution)/shard_map/ppermute | solution.py:17
  101.3 16.3 %copy-start = (bf16[1,1024,576]{2,1,0:T(8,128)(2,1)S(1)}, bf16[1,1024,576]{2,1,0:T(8,128)(2,1)}, u32[]{:S(2)}) copy-start(bf16[1,1024,576]{2,1,0:T(8,128)(2,1)} %all-gather.5.cloned.1.call-done) | copy-start | bytes 3538948
  157.5 19.6 %copy-start.3 = (f32[64,576]{1,0:T(8,128)}, f32[64,576]{1,0:T(8,128)S(1)}, u32[]{:S(2)}) copy-start(f32[64,576]{1,0:T(8,128)S(1)} %fusion.196) | copy-start | bytes 442372
  159.1 18.1 %copy-start.77 = (f32[64]{0:T(128)}, f32[64]{0:T(128)S(1)}, u32[]{:S(2)}) copy-start(f32[64]{0:T(128)S(1)} %fusion.265) | copy-start | bytes 772
  159.1 16.2 %copy-start.78 = (f32[64]{0:T(128)}, f32[64]{0:T(128)S(1)}, u32[]{:S(2)}) copy-start(f32[64]{0:T(128)S(1)} %fusion.264) | copy-start | bytes 772
  159.6 14.7 %copy-start.28 = (bf16[64,2,256]{2,0,1:T(8,128)(2,1)}, bf16[64,2,256]{2,0,1:T(8,128)(2,1)S(1)}, u32[]{:S(2)}) copy-start(bf16[64,2,256]{2,0,1:T(8,128)(2,1)S(1)} %fusion.231) | copy-start | bytes 196612
  159.9 15.9 %copy-start.30 = (bf16[64,2,256]{2,0,1:T(8,128)(2,1)}, bf16[64,2,256]{2,0,1:T(8,128)(2,1)S(1)}, u32[]{:S(2)}) copy-start(bf16[64,2,256]{2,0,1:T(8,128)(2,1)S(1)} %fusion.219) | copy-start | bytes 196612
  160.2 11.0 %copy-start.12 = (bf16[2,64,1024]{2,1,0:T(8,128)(2,1)S(1)}, bf16[2,64,1024]{2,1,0:T(8,128)(2,1)}, u32[]{:S(2)}) copy-start(bf16[2,64,1024]{2,1,0:T(8,128)(2,1)} %param.15) | copy-start | bytes 786436
  160.4 10.9 %copy-start.10 = (bf16[64,1024]{1,0:T(8,128)(2,1)S(1)}, bf16[64,1024]{1,0:T(8,128)(2,1)}, u32[]{:S(2)}) copy-start(bf16[64,1024]{1,0:T(8,128)(2,1)} %copy-done.9) | copy-start | bytes 393220
  161.1 15.1 %copy-start.61 = (f32[2,64]{1,0:T(2,128)}, f32[2,64]{1,0:T(2,128)S(1)}, u32[]{:S(2)}) copy-start(f32[2,64]{1,0:T(2,128)S(1)} %get-tuple-element.211) | copy-start | bytes 1540
  161.1 15.1 %copy-start.63 = (f32[2,64]{1,0:T(2,128)}, f32[2,64]{1,0:T(2,128)S(1)}, u32[]{:S(2)}) copy-start(f32[2,64]{1,0:T(2,128)S(1)} %get-tuple-element.118) | copy-start | bytes 1540
  161.2 15.0 %copy-start.65 = (f32[2,64]{1,0:T(2,128)}, f32[2,64]{1,0:T(2,128)S(1)}, u32[]{:S(2)}) copy-start(f32[2,64]{1,0:T(2,128)S(1)} %fusion.243) | copy-start | bytes 1540
  162.2 9.1 %collective-permute-start.1 = (bf16[64,1024]{1,0:T(8,128)(2,1)S(1)}, bf16[64,1024]{1,0:T(8,128)(2,1)S(1)}, u32[]{:S(2)}, u32[]{:S(2)}) collective-permute-start(bf16[64,1024]{1,0:T(8,128)(2,1)S(1)} %fusion.178), channel_id=1, source_target_pairs={{16,0},{17,1},{18,2},{19,3},{20,4},{21,5},{22,6},{23,7},{24,8},{25... | collective-permute-start | bytes 393224 | tf_op jit(solution)/shard_map/ppermute | solution.py:17
  163.7 12.5 %copy-start.67 = (f32[2,64]{1,0:T(2,128)}, f32[2,64]{1,0:T(2,128)S(1)}, u32[]{:S(2)}) copy-start(f32[2,64]{1,0:T(2,128)S(1)} %fusion.244) | copy-start | bytes 1540
  178.4 48.7 %reduce-scatter.11.cloned.1.call-start = ((), (), s32[]{:S(2)}) async-start(), calls=%async_computation.9 | async-start | bytes 655360 | tf_op jit(solution)/shard_map/reduce_scatter | solution.py:164
  183.2 67.6 %reduce-scatter.7.cloned.1.call-start = ((), (), s32[]{:S(2)}) async-start(), calls=%async_computation.6 | async-start | bytes 1474560 | tf_op jit(solution)/shard_map/reduce_scatter | solution.py:155
  186.3 88.4 %reduce-scatter.5.cloned.1.call-start = ((), (), s32[]{:S(2)}) async-start(), calls=%async_computation.5 | async-start | bytes 983040 | tf_op jit(solution)/shard_map/reduce_scatter | solution.py:152
  205.1 18.7 %copy-start.105 = (f32[16]{0:T(128)S(1)}, f32[16]{0:T(128)}, u32[]{:S(2)}) copy-start(f32[16]{0:T(128)} %dynamic-slice.7) | copy-start | bytes 196
  205.1 19.6 %copy-start.52 = (bf16[16,1024]{1,0:T(8,128)(2,1)S(1)}, bf16[16,1024]{1,0:T(8,128)(2,1)}, u32[]{:S(2)}) copy-start(bf16[16,1024]{1,0:T(8,128)(2,1)} %constant_dynamic-slice_fusion) | copy-start | bytes 98308
  205.1 19.6 %copy-start.53 = (bf16[16,1024]{1,0:T(8,128)(2,1)S(1)}, bf16[16,1024]{1,0:T(8,128)(2,1)}, u32[]{:S(2)}) copy-start(bf16[16,1024]{1,0:T(8,128)(2,1)} %constant_dynamic-slice_fusion.1) | copy-start | bytes 98308
  205.1 19.6 %copy-start.88 = (pred[2]{0:T(512)(128)(4,1)S(1)}, pred[2]{0:T(512)(128)(4,1)}, u32[]{:S(2)}) copy-start(pred[2]{0:T(512)(128)(4,1)} %get-tuple-element.235) | copy-start | bytes 10
  205.1 19.6 %copy-start.90 = (pred[2]{0:T(512)(128)(4,1)S(1)}, pred[2]{0:T(512)(128)(4,1)}, u32[]{:S(2)}) copy-start(pred[2]{0:T(512)(128)(4,1)} %get-tuple-element.236) | copy-start | bytes 10
  205.1 19.6 %copy-start.98 = (pred[2]{0:T(512)(128)(4,1)S(1)}, pred[2]{0:T(512)(128)(4,1)}, u32[]{:S(2)}) copy-start(pred[2]{0:T(512)(128)(4,1)} %iota_compare_fusion.10) | copy-start | bytes 10
  206.5 102.4 %all-reduce.56.cloned.1.call-start = ((), (), s32[]{:S(2)}) async-start(), calls=%async_computation.7 | async-start | bytes 589824 | tf_op jit(solution)/shard_map/psum | solution.py:172
  (87 other events, 252.3 us)
Sparse Core Ops, SparseCore 0:
  10.1 43.3 all-gather.4
  178.5 20.0 reduce-scatter.8
  200.9 20.1 reduce-scatter.10
  223.2 27.5 reduce-scatter.6
  252.9 21.7 reduce-scatter.4
  276.9 31.9 all-reduce.55
